TPU v7x, 32 devices: a whole 2x2x4 slice. The times are simulated.
32 devices in a mesh: grp: 2 (over y), seq: 4 (over z), head: 4 (over x, core).
Axes of the slice: x: 2, y: 2, z: 4, core: 2. Of those that a mesh axis runs over, the one named last changes fastest.
Arguments:
- draft_features: bfloat16 [2048, 8192], P(('grp', 'seq'), 'head'), parts along dimension 0, may hold values from -6 to 6
- w_key: bfloat16 [8192, 1024], P(None, 'head'), may hold values from -0.0625 to 0.0625
- w_value: bfloat16 [8192, 1024], P(None, 'head'), may hold values from -0.0625 to 0.0625
- accepted: int32 [256], P(('grp', 'seq')), parts along dimension 0, may hold values from 1 to 8
- owner_group: int32 [256], P(('grp', 'seq')), parts along dimension 0, may hold values from 0 to 3, as said below
- page_slot: int32 [256], P(('grp', 'seq')), parts along dimension 0, may hold values from 0 to 63, as said below
Outputs:
- key_cache: bfloat16 [512, 8, 1024], P(('grp', 'seq'), None, 'head'), parts along dimension 0
- value_cache: bfloat16 [512, 8, 1024], P(('grp', 'seq'), None, 'head'), parts along dimension 0
There are 2 independent parts, one for each index of `grp`. A program takes and returns all parts, laid end to end along the dimension named above; an argument that names none is the same for every part. Nothing has to cross between parts.
Inputs may be any that keep to these rules, and one draw needn't show every extreme that they name: `owner_group`: the requests of one index of seq go to exactly 2 distinct owners, 16 to each; some owner receives 64 requests. `page_slot`: the requests of one owner have distinct slots.
All inputs are finite; a program needn't handle non-finite values.
Results may differ from a plain program's by a relative error of at most 0.001.
Values may be sent and summed in bfloat16 or wider, within the bound.
A program may use at most 64 MiB of HBM per device.

v0:
```python
import jax
import jax.numpy as jnp
from jax import lax
from jax.sharding import PartitionSpec as P


def pair_slots(owner_ids, slot_cap):
    row_count = owner_ids.shape[-1]
    same_owner = owner_ids[..., :, None] == owner_ids[..., None, :]
    before = lax.broadcasted_iota(jnp.int32, (row_count, row_count), 1) < lax.broadcasted_iota(
        jnp.int32, (row_count, row_count), 0
    )
    within = jnp.sum(jnp.where(same_owner & before, 1, 0), axis=-1).astype(jnp.int32)
    return owner_ids * slot_cap + within


def one_hot(labels, columns):
    return (
        labels[:, None] == lax.broadcasted_iota(jnp.int32, (labels.shape[0], columns), 1)
    ).astype(jnp.bfloat16)


def pack_rows(payload, slot_ids, slot_total):
    select = one_hot(slot_ids, slot_total)
    packed = lax.dot_general(
        select, payload, (((0,), (0,)), ((), ())), preferred_element_type=jnp.float32
    )
    return packed.astype(jnp.bfloat16)


def placement(all_owner, all_page, owner_self, req_dev, slot_cap, seq_count):
    slot_total = slot_cap * seq_count
    slot_ids = pair_slots(all_owner.reshape(seq_count, req_dev), slot_cap).reshape(-1)
    source = lax.broadcasted_iota(jnp.int32, (seq_count, req_dev), 0).reshape(-1)
    column = source * slot_cap + slot_ids - all_owner * slot_cap
    target = jnp.where(all_owner == owner_self, all_page, -1)
    to_page = one_hot(target, slot_total)
    from_column = one_hot(column, slot_total)
    placing = lax.dot_general(
        to_page, from_column, (((0,), (0,)), ((), ())), preferred_element_type=jnp.float32
    )
    return placing.astype(jnp.bfloat16)


def local(draft_features, w_key, w_value, accepted, owner_group, page_slot):
    req_dev = accepted.shape[0]
    draft_rows = draft_features.shape[0] // req_dev
    head_cols = w_key.shape[1]
    seq_count = lax.axis_size("seq")
    owner_self = lax.axis_index("seq")
    slot_cap = max(2, 2 * req_dev // seq_count)
    slot_total = slot_cap * seq_count
    send_slots = pair_slots(owner_group, slot_cap)
    live_rows = lax.broadcasted_iota(jnp.int32, (req_dev, draft_rows), 1) < accepted[:, None]
    all_owner, all_page = (
        lax.all_gather(owner_group, "seq", axis=0, tiled=True),
        lax.all_gather(page_slot, "seq", axis=0, tiled=True),
    )
    placing = placement(all_owner, all_page, owner_self, req_dev, slot_cap, seq_count)
    portion = lax.all_gather(draft_features, "head", axis=1, tiled=True)
    key_sum = jnp.dot(portion, w_key, preferred_element_type=jnp.float32)
    value_sum = jnp.dot(portion, w_value, preferred_element_type=jnp.float32)
    key_local = jnp.where(
        live_rows[:, :, None], key_sum.reshape(req_dev, draft_rows, head_cols), 0.0
    )
    value_local = jnp.where(
        live_rows[:, :, None], value_sum.reshape(req_dev, draft_rows, head_cols), 0.0
    )
    key_local = key_local.astype(jnp.bfloat16).reshape(req_dev, draft_rows * head_cols)
    value_local = value_local.astype(jnp.bfloat16).reshape(req_dev, draft_rows * head_cols)
    key_send = pack_rows(key_local, send_slots, slot_total)
    value_send = pack_rows(value_local, send_slots, slot_total)
    key_arrived, value_arrived = (
        lax.all_to_all(key_send, "seq", split_axis=0, concat_axis=0, tiled=True),
        lax.all_to_all(value_send, "seq", split_axis=0, concat_axis=0, tiled=True),
    )
    key_cache = jnp.dot(placing, key_arrived, preferred_element_type=jnp.float32).astype(
        jnp.bfloat16
    )
    value_cache = jnp.dot(placing, value_arrived, preferred_element_type=jnp.float32).astype(
        jnp.bfloat16
    )
    return (
        key_cache.reshape(slot_total, draft_rows, head_cols),
        value_cache.reshape(slot_total, draft_rows, head_cols),
    )


def solution(mesh):
    placed = (
        P(("grp", "seq"), "head"),
        P(None, "head"),
        P(None, "head"),
        P(("grp", "seq")),
        P(("grp", "seq")),
        P(("grp", "seq")),
    )
    return jax.shard_map(
        local,
        mesh=mesh,
        in_specs=placed,
        out_specs=(P(("grp", "seq"), None, "head"), P(("grp", "seq"), None, "head")),
        check_vma=False,
    )
```

profile of v0, /device:TPU:0, one launch (start us, length us, event | category | flops | bytes accessed | tf_op | source)
XLA Modules:
  0.0 84.7 jit_solution(431942104099704447)
XLA Ops:
  7.2 0.0 all-gather.2.cloned.1.call-start
  7.2 0.7 all-gather.2.cloned.1.call-update
  7.9 1.2 %dynamic-slice = u32[1]{0:T(128)} dynamic-slice(u32[32]{0:T(128)} %constant.19, u32[]{:T(128)S(6)} %add.13), dynamic_slice_sizes={1} | dynamic-slice | bytes 12
  9.8 0.9 %dynamic-update-slice = s32[128]{0:T(128)S(1)} dynamic-update-slice(s32[128]{0:T(128)S(1)} %broadcast.31.clone, s32[32]{0:T(128)} %param.10, u32[]{:T(128)} %bitcast) | dynamic-update-slice | bytes 260
  10.7 0.8 dynamic-update-slice.1
  11.5 9.9 %all-reduce.2 = (s32[128]{0:T(128)S(1)}, s32[128]{0:T(128)S(1)}) all-reduce(s32[128]{0:T(128)S(1)} %dynamic-update-slice, s32[128]{0:T(128)S(1)} %dynamic-update-slice.1), channel_id=1, replica_groups=mesh['grp'=2,'seq'=4,'head'=4] {'seq'}, use_global_device_ids=true, to_apply=%add | all-reduce | flops 256 | bytes 2048
  21.4 0.1 eq.66
  21.5 0.1 mul.19
  21.6 0.2 select_reduce_fusion
  21.8 0.1 reduce_sum.21
  21.9 0.7 iota_compare_fusion.4
  22.7 0.1 broadcast_in_dim.53
  22.8 0.9 %select_reduce_fusion.1 = s32[32]{0:T(128)S(1)} fusion(s32[32]{0:T(128)} %param.10), kind=kLoop, calls=%fused_computation.16 | loop fusion | flops 5088 | bytes 256 | tf_op jit(solution)/shard_map/reduce_sum | solution.py:13
  23.7 0.7 multiply_add_fusion
  24.4 22.4 %all-gather.2.cloned.1.call-done = bf16[256,8192]{1,0:T(8,128)(2,1)} async-done(((bf16[256,2048]{1,0:T(8,128)(2,1)}), bf16[256,8192]{1,0:T(8,128)(2,1)}) %all-gather.2.cloned.1.call-update) | async-done | bytes 4194320 | tf_op jit(solution)/shard_map/all_gather | solution.py:60
  46.7 4.7 %fusion.9 = bf16[256,256]{1,0:T(8,128)(2,1)S(1)} fusion(bf16[256,8192]{1,0:T(8,128)(2,1)} %all-gather.2.cloned.1.call-done, bf16[8192,256]{1,0:T(8,128)(2,1)} %param.8), kind=kOutput, calls=%fused_computation.27 | convolution fusion | flops 1073741824 | bytes 8519680 | tf_op jit(solution)/shard_map/dot_general | solution.py:62
  51.5 0.1 reshape.67
  51.5 1.1 %convolution_convert_fusion.1 = bf16[64,2048]{1,0:T(8,128)(2,1)} fusion(pred[32,2048]{1,0:T(8,128)(4,1)S(1)} %bitcast.23, bf16[32,2048]{1,0:T(8,128)(2,1)S(1)} %reshape.67, s32[32]{0:T(128)S(1)} %multiply_add_fusion), kind=kOutput, calls=%fused_computation.1 | convolution fusion | flops 8587264 | bytes 458880 | tf_op jit(solution)/shard_map/dot_general | solution.py:25
  52.6 4.7 %all-to-all-start.1 = ((bf16[4,16,2048]{2,1,0:T(8,128)(2,1)}), bf16[4,16,2048]{2,1,0:T(8,128)(2,1)S(1)}, u32[]{:S(2)}, u32[]{:S(2)}) async-start(bf16[4,16,2048]{2,1,0:T(8,128)(2,1)} %bitcast.3), calls=%async_computation.1 | async-start | bytes 524288 | tf_op jit(solution)/shard_map/all_to_all | solution.py:75
  57.2 4.7 %fusion.8 = bf16[256,256]{1,0:T(8,128)(2,1)S(1)} fusion(bf16[256,8192]{1,0:T(8,128)(2,1)} %all-gather.2.cloned.1.call-done, bf16[8192,256]{1,0:T(8,128)(2,1)} %param.7), kind=kOutput, calls=%fused_computation.26 | convolution fusion | flops 1073741824 | bytes 8519680 | tf_op jit(solution)/shard_map/dot_general | solution.py:61
  62.0 0.1 reshape.65
  62.0 1.1 %convolution_convert_fusion.3 = bf16[64,2048]{1,0:T(8,128)(2,1)} fusion(pred[32,2048]{1,0:T(8,128)(4,1)S(1)} %bitcast.24, bf16[32,2048]{1,0:T(8,128)(2,1)S(1)} %reshape.65, s32[32]{0:T(128)S(1)} %multiply_add_fusion), kind=kOutput, calls=%fused_computation.3 | convolution fusion | flops 8587264 | bytes 458880 | tf_op jit(solution)/shard_map/dot_general | solution.py:25
  63.1 3.5 %all-to-all-done.1 = bf16[4,16,2048]{2,1,0:T(8,128)(2,1)S(1)} async-done(((bf16[4,16,2048]{2,1,0:T(8,128)(2,1)}), bf16[4,16,2048]{2,1,0:T(8,128)(2,1)S(1)}, u32[]{:S(2)}, u32[]{:S(2)}) %all-to-all-start.1) | async-done | bytes 262176 | tf_op jit(solution)/shard_map/all_to_all | solution.py:75
  66.6 3.4 %all-to-all-start = ((bf16[4,16,2048]{2,1,0:T(8,128)(2,1)}), bf16[4,16,2048]{2,1,0:T(8,128)(2,1)S(1)}, u32[]{:S(2)}, u32[]{:S(2)}) async-start(bf16[4,16,2048]{2,1,0:T(8,128)(2,1)} %bitcast.1), calls=%async_computation | async-start | bytes 524288 | tf_op jit(solution)/shard_map/all_to_all | solution.py:74
  70.0 0.3 convolution_convert_fusion.4
  70.2 0.2 convolution_convert_fusion
  70.5 0.8 copy.10
  71.2 5.7 %all-to-all-done = bf16[4,16,2048]{2,1,0:T(8,128)(2,1)S(1)} async-done(((bf16[4,16,2048]{2,1,0:T(8,128)(2,1)}), bf16[4,16,2048]{2,1,0:T(8,128)(2,1)S(1)}, u32[]{:S(2)}, u32[]{:S(2)}) %all-to-all-start) | async-done | bytes 262176 | tf_op jit(solution)/shard_map/all_to_all | solution.py:74
  76.9 0.2 convolution_convert_fusion.2
  77.1 0.8 copy.9
  (6 shorter events, 0.1 us)
Async XLA Ops:
  7.2 39.6 %all-gather.2.cloned.1.call-start = ((), (), s32[]{:S(2)}) async-start(), calls=%async_computation.2 | async-start | bytes 5242880 | tf_op jit(solution)/shard_map/all_gather | solution.py:60
  52.6 14.0 %all-to-all-start.1 = ((bf16[4,16,2048]{2,1,0:T(8,128)(2,1)}), bf16[4,16,2048]{2,1,0:T(8,128)(2,1)S(1)}, u32[]{:S(2)}, u32[]{:S(2)}) async-start(bf16[4,16,2048]{2,1,0:T(8,128)(2,1)} %bitcast.3), calls=%async_computation.1 | async-start | bytes 524288 | tf_op jit(solution)/shard_map/all_to_all | solution.py:75
  66.6 10.3 %all-to-all-start = ((bf16[4,16,2048]{2,1,0:T(8,128)(2,1)}), bf16[4,16,2048]{2,1,0:T(8,128)(2,1)S(1)}, u32[]{:S(2)}, u32[]{:S(2)}) async-start(bf16[4,16,2048]{2,1,0:T(8,128)(2,1)} %bitcast.1), calls=%async_computation | async-start | bytes 524288 | tf_op jit(solution)/shard_map/all_to_all | solution.py:74
Sparse Core Ops, SparseCore 0:
  9.5 37.1 all-gather.1
where the time goes:
time: 85.1 us; the launch traced here: 84.7 us
  waiting for transfers between devices  32.2 us (38%)
  between operations  14.8 us (17%)
  matrix products  12.2 us (14%)
  blocking collectives  9.92 us (12%)
  starting transfers between devices  8.1 us (10%)
  local copies, waits for them, and re-layouts  4.98 us (6%)
  other arithmetic  2.55 us (3%)
    all_gather x1, waiting for transfers between devices, local(): portion = lax.all_gather(draft_features, 'head', axis=1, tiled=True)  22.4 us
    unnamed x1, blocking collectives  9.92 us
    all_to_all x1, waiting for transfers between devices, local(): lax.all_to_all(key_send, 'seq', split_axis=0, concat_axis=0, tiled=True)  5.69 us
    dot_general x1, matrix products, local(): value_sum = jnp.dot(portion, w_value, preferred_element_type=jnp.float32)  4.71 us
    dot_general x1, matrix products, local(): key_sum = jnp.dot(portion, w_key, preferred_element_type=jnp.float32)  4.71 us
    all_to_all x1, starting transfers between devices, local(): lax.all_to_all(value_send, 'seq', split_axis=0, concat_axis=0, tiled=True)  4.65 us
    unnamed x8, local copies, waits for them, and re-layouts  4.49 us
    all_to_all x1, waiting for transfers between devices, local(): lax.all_to_all(value_send, 'seq', split_axis=0, concat_axis=0, tiled=True)  3.47 us
  transfers between devices with their start and end apart: 3, of which 3 were waited for; matrix products, arithmetic and copies ran while one was open for 15% of the time, Pallas kernels for 0%

commit v1 on v0

--- a/solution.py
+++ b/solution.py
@@ -1,7 +1,13 @@
+import functools
+
 import jax
 import jax.numpy as jnp
 from jax import lax
+from jax.experimental import pallas as pl
+from jax.experimental.pallas import tpu as pltpu
 from jax.sharding import PartitionSpec as P
+
+MESH = pl.DeviceIdType.MESH
 
 
 def pair_slots(owner_ids, slot_cap):
@@ -42,7 +48,7 @@
     return placing.astype(jnp.bfloat16)
 
 
-def local(draft_features, w_key, w_value, accepted, owner_group, page_slot):
+def plain(draft_features, w_key, w_value, accepted, owner_group, page_slot):
     req_dev = accepted.shape[0]
     draft_rows = draft_features.shape[0] // req_dev
     head_cols = w_key.shape[1]
@@ -86,6 +92,229 @@
     )
 
 
+def kernel(
+    dims, f_hbm, wk_hbm, wv_hbm, acc_ref, own_ref, page_ref, k_out, v_out,
+    feats, weights, part, rows_buf, keys, place, k_stage, v_stage,
+    load_sem, w_sem, out_sem, x_send, x_recv, d_send, d_recv, f_send, f_recv,
+    z_send, z_recv, i_send, i_recv,
+):
+    seqs, chunks, draft = dims
+    rows, depth = f_hbm.shape
+    cols = wk_hbm.shape[1]
+    step = rows // chunks
+    requests = rows // draft
+    slot_rows = k_stage.shape[0]
+    head = lax.axis_index("head")
+    seq = lax.axis_index("seq")
+    partner = head + 1 - 2 * (head % 2)
+    across = (head + 2) % 4
+    blocks = (head, partner, across, (partner + 2) % 4)
+
+    load = pltpu.make_async_copy(f_hbm, feats.at[0], load_sem)
+    load.start()
+    w_loads = []
+    for k in range(4):
+        at = pl.ds(pl.multiple_of(blocks[k] * depth, depth), depth)
+        for n, w in enumerate((wk_hbm, wv_hbm)):
+            w_loads.append(
+                pltpu.make_async_copy(
+                    w.at[at, :], weights.at[k, :, pl.ds(n * cols, cols)], w_sem.at[k, n]
+                )
+            )
+
+    barrier = pltpu.get_barrier_semaphore()
+    peers = [{"head": partner}, {"head": across}]
+    peers += [{"seq": (seq + d) % seqs} for d in range(1, seqs)]
+    for peer in peers:
+        pl.semaphore_signal(barrier, inc=1, device_id=peer, device_id_type=MESH)
+    for w_load in w_loads:
+        w_load.start()
+    load.wait()
+    pl.semaphore_wait(barrier, len(peers))
+
+    def remote(src, dst, send_sem, recv_sem, peer):
+        return pltpu.make_async_remote_copy(
+            src_ref=src, dst_ref=dst, send_sem=send_sem, recv_sem=recv_sem,
+            device_id=peer, device_id_type=MESH,
+        )
+
+    def cut(c):
+        return pl.ds(c * step, step)
+
+    def x_copy(c):
+        return remote(
+            feats.at[0, cut(c), :], feats.at[2, cut(c), :], x_send.at[c], x_recv.at[c],
+            {"head": across},
+        )
+
+    def forward(c):
+        return remote(
+            feats.at[2, cut(c), :], feats.at[3, cut(c), :], f_send.at[c], f_recv.at[c],
+            {"head": partner},
+        )
+
+    def z_copy(c, d):
+        return remote(
+            rows_buf.at[0, cut(c), :], rows_buf.at[d, cut(c), :],
+            z_send.at[d - 1, c], z_recv.at[d - 1, c], {"seq": (seq + d) % seqs},
+        )
+
+    def i_copy(d):
+        return remote(
+            keys.at[0], keys.at[d], i_send.at[d - 1], i_recv.at[d - 1],
+            {"seq": (seq + d) % seqs},
+        )
+
+    for c in range(chunks):
+        x_copy(c).start()
+    own = remote(feats.at[0], feats.at[1], d_send, d_recv, {"head": partner})
+    own.start()
+
+    spread = (
+        lax.broadcasted_iota(jnp.int32, (requests, rows), 1) // draft
+        == lax.broadcasted_iota(jnp.int32, (requests, rows), 0)
+    ).astype(jnp.bfloat16)
+
+    def widen(ref):
+        values = jnp.broadcast_to(ref[...].astype(jnp.float32), (8, requests))
+        wide = jnp.dot(
+            values.astype(jnp.bfloat16), spread, preferred_element_type=jnp.float32
+        )
+        return wide.astype(jnp.int32)
+
+    within = lax.broadcasted_iota(jnp.int32, (8, rows), 1) % draft
+    keys[0] = jnp.where(
+        within < widen(acc_ref),
+        widen(own_ref) * slot_rows + widen(page_ref) * draft + within,
+        -1,
+    )
+    for d in range(1, seqs):
+        i_copy(d).start()
+
+    w_loads[0].wait()
+    w_loads[1].wait()
+    part[...] = jnp.dot(feats[0], weights[0], preferred_element_type=jnp.float32)
+    own.wait_recv()
+    w_loads[2].wait()
+    w_loads[3].wait()
+    part[...] += jnp.dot(feats[1], weights[1], preferred_element_type=jnp.float32)
+
+    for d in range(seqs):
+        if d > 0:
+            i_copy(d).wait_recv()
+        target = keys[d][0:1, :] - seq * slot_rows
+        place[d] = (
+            lax.broadcasted_iota(jnp.int32, (slot_rows, rows), 0) == target
+        ).astype(jnp.bfloat16)
+    for w_load in w_loads[4:]:
+        w_load.wait()
+
+    @pl.loop(0, chunks)
+    def _(c):
+        at = cut(pl.multiple_of(c, 1))
+        x_copy(c).wait_recv()
+        forward(c).start()
+        total = part[at, :] + jnp.dot(
+            feats[2, at, :], weights[2], preferred_element_type=jnp.float32
+        )
+        forward(c).wait_recv()
+        total += jnp.dot(feats[3, at, :], weights[3], preferred_element_type=jnp.float32)
+        rows_buf[0, at, :] = total.astype(jnp.bfloat16)
+        for d in range(1, seqs):
+            z_copy(c, d).start()
+
+    half = rows // 2
+
+    def placed(h):
+        total = None
+        for d in range(seqs):
+            more = jnp.dot(
+                place[d, :, h * half : (h + 1) * half],
+                rows_buf[d, h * half : (h + 1) * half, :],
+                preferred_element_type=jnp.float32,
+            )
+            total = more if total is None else total + more
+        return total
+
+    def arrive(first, last):
+        @pl.loop(first, last)
+        def _(c):
+            for d in range(1, seqs):
+                z_copy(c, d).wait_recv()
+
+    arrive(0, chunks // 2)
+    first = placed(0)
+    arrive(chunks // 2, chunks)
+    cache = (first + placed(1)).astype(jnp.bfloat16)
+    k_stage[...] = cache[:, :cols]
+    v_stage[...] = cache[:, cols:]
+    outs = [
+        pltpu.make_async_copy(k_stage, k_out, out_sem.at[0]),
+        pltpu.make_async_copy(v_stage, v_out, out_sem.at[1]),
+    ]
+    for out in outs:
+        out.start()
+
+    @pl.loop(0, chunks)
+    def _(c):
+        x_copy(c).wait_send()
+        forward(c).wait_send()
+        for d in range(1, seqs):
+            z_copy(c, d).wait_send()
+
+    own.wait_send()
+    for d in range(1, seqs):
+        i_copy(d).wait_send()
+    for out in outs:
+        out.wait()
+
+
+def fused(seqs, draft_features, w_key, w_value, accepted, owner_group, page_slot):
+    rows, depth = draft_features.shape
+    cols = w_key.shape[1]
+    requests = accepted.shape[0]
+    draft = rows // requests
+    slots = max(2, 2 * requests // seqs) * seqs
+    chunks = 8
+    step = rows // chunks
+    dma = pltpu.SemaphoreType.DMA
+    any_spec = pl.BlockSpec(memory_space=pl.ANY)
+    vmem_spec = pl.BlockSpec(memory_space=pltpu.VMEM)
+    bf16 = jnp.bfloat16
+    key_cache, value_cache = pl.pallas_call(
+        functools.partial(kernel, (seqs, chunks, draft)),
+        out_shape=(jax.ShapeDtypeStruct((slots * draft, cols), bf16),) * 2,
+        in_specs=[any_spec] * 3 + [vmem_spec] * 3,
+        out_specs=(any_spec, any_spec),
+        scratch_shapes=[
+            pltpu.VMEM((4, rows, depth), bf16),
+            pltpu.VMEM((4, depth, 2 * cols), bf16),
+            pltpu.VMEM((rows, 2 * cols), jnp.float32),
+            pltpu.VMEM((seqs, rows, 2 * cols), bf16),
+            pltpu.VMEM((seqs, 8, rows), jnp.int32),
+            pltpu.VMEM((seqs, slots * draft, rows), bf16),
+            pltpu.VMEM((slots * draft, cols), bf16),
+            pltpu.VMEM((slots * draft, cols), bf16),
+            dma, dma((4, 2)), dma((2,)),
+            dma((chunks,)), dma((chunks,)), dma, dma, dma((chunks,)), dma((chunks,)),
+            dma((seqs - 1, chunks)), dma((seqs - 1, chunks)),
+            dma((seqs - 1,)), dma((seqs - 1,)),
+        ],
+        compiler_params=pltpu.CompilerParams(
+            collective_id=0, has_side_effects=True, vmem_limit_bytes=48 << 20
+        ),
+        name="import_rows",
+    )(
+        draft_features, w_key, w_value,
+        accepted.reshape(1, requests), owner_group.reshape(1, requests),
+        page_slot.reshape(1, requests),
+    )
+    return (
+        key_cache.reshape(slots, draft, cols),
+        value_cache.reshape(slots, draft, cols),
+    )
+
+
 def solution(mesh):
     placed = (
         P(("grp", "seq"), "head"),
@@ -95,6 +324,8 @@
         P(("grp", "seq")),
         P(("grp", "seq")),
     )
+    seqs = mesh.shape["seq"]
+    local = functools.partial(fused, seqs) if mesh.shape["head"] == 4 else plain
     return jax.shard_map(
         local,
         mesh=mesh,

time: 85.1 us -> 45 us (0.53)
  Pallas kernels: 0 us -> 37.3 us
  waiting for transfers between devices: 32.2 us -> 0 us
  between operations: 14.8 us -> 0.65 us
  matrix products: 12.2 us -> 0 us
  blocking collectives: 9.92 us -> 0 us
  starting transfers between devices: 8.1 us -> 0 us
  other arithmetic: 2.55 us -> 0 us
  local copies, waits for them, and re-layouts: 4.98 us -> 6.78 us
    pallas_call x0 -> x1, Pallas kernels: none -> 37.3 us  [fused(): pl.pallas_call(functools.partial(kernel, (seqs, chunks, draft)), out_shap...]
    all_gather x1 -> x0, waiting for transfers between devices: 22.4 us -> none  [local(): portion = lax.all_gather(draft_features, 'head', axis=1, tiled=True)]
    dot_general x7 -> x0, matrix products: 12.2 us -> none  [the longest x1 4.71 us: local(): value_sum = jnp.dot(portion, w_value, preferred_element_type=jnp.float32)]
    unnamed x1 -> x0, blocking collectives: 9.92 us -> none
    all_to_all x2 -> x0, waiting for transfers between devices: 9.16 us -> none  [the longest x1 5.69 us: local(): lax.all_to_all(key_send, 'seq', split_axis=0, concat_axis=0, tiled=True)]
    all_to_all x2 -> x0, starting transfers between devices: 8.06 us -> none  [the longest x1 4.65 us: local(): lax.all_to_all(value_send, 'seq', split_axis=0, concat_axis=0, tiled=True)]
    unnamed x8 -> x12, local copies, waits for them, and re-layouts: 4.49 us -> 6.78 us
    reduce_sum x2 -> x0, other arithmetic: 1.13 us -> none  [pair_slots(): jnp.sum(jnp.where(same_owner & before, 1, 0), axis=-1).astype(jnp.int32)]
  transfers between devices with their start and end apart: 3 -> 0, of which waited for: 3 -> 0; matrix products, arithmetic and copies ran while one was open for 15% -> 0% of each run, Pallas kernels for 0% -> 0%
where the time goes in v1:
time: 45 us; the launch traced here: 44.8 us
  Pallas kernels  37.3 us (83%)
  local copies, waits for them, and re-layouts  6.78 us (15%)
  between operations  0.65 us (1%)
    pallas_call x1, Pallas kernels, fused(): pl.pallas_call(functools.partial(kernel, (seqs, chunks, draft)), out_shap...  37.3 us
    unnamed x12, local copies, waits for them, and re-layouts  6.78 us

profile of v1, /device:TPU:0, one launch (start us, length us, event | category | flops | bytes accessed | tf_op | source)
XLA Modules:
  0.0 44.8 jit_solution(16359119430889407645)
XLA Ops:
  0.6 0.0 copy-start
  0.6 2.2 %copy-done = bf16[8192,256]{1,0:T(8,128)(2,1)S(1)} copy-done((bf16[8192,256]{1,0:T(8,128)(2,1)S(1)}, bf16[8192,256]{1,0:T(8,128)(2,1)}, u32[]{:S(2)}) %copy-start) | copy-done | bytes 4194328
  2.8 0.0 copy-start.1
  2.8 1.2 %copy-done.1 = bf16[256,2048]{1,0:T(8,128)(2,1)S(1)} copy-done((bf16[256,2048]{1,0:T(8,128)(2,1)S(1)}, bf16[256,2048]{1,0:T(8,128)(2,1)}, u32[]{:S(2)}) %copy-start.1) | copy-done | bytes 1048600
  4.0 0.0 copy-start.2
  4.0 0.7 %copy-done.2 = s32[32]{0:T(128)S(1)} copy-done((s32[32]{0:T(128)S(1)}, s32[32]{0:T(128)}, u32[]{:S(2)}) %copy-start.2) | copy-done | bytes 152
  4.7 0.0 copy-start.3
  4.7 0.7 %copy-done.3 = s32[32]{0:T(128)S(1)} copy-done((s32[32]{0:T(128)S(1)}, s32[32]{0:T(128)}, u32[]{:S(2)}) %copy-start.3) | copy-done | bytes 152
  5.4 0.0 copy-start.4
  5.4 0.7 %copy-done.4 = s32[32]{0:T(128)S(1)} copy-done((s32[32]{0:T(128)S(1)}, s32[32]{0:T(128)}, u32[]{:S(2)}) %copy-start.4) | copy-done | bytes 152
  6.0 37.3 %import_rows.1 = (bf16[512,256]{1,0:T(8,128)(2,1)S(1)}, bf16[512,256]{1,0:T(8,128)(2,1)S(1)}) custom-call(bf16[256,2048]{1,0:T(8,128)(2,1)S(1)} %copy-done.1, bf16[8192,256]{1,0:T(8,128)(2,1)S(1)} %copy-done, bf16[8192,256]{1,0:T(8,128)(2,1)} %wv_hbm.1, s32[1,32]{1,0:T(1,128)S(1)} %bitcast.7, s32[1,32]{1,0:T(1,128)S(1)} %bitcast.8, s32[1,32]{1,0:T(1,128)S(1)} %bitcast.9), custom_call_target="tpu_custom_call" | custom-call | tf_op jit(solution)/shard_map/import_rows/pallas_call | solution.py:284
  43.4 0.7 %copy.10 = bf16[64,8,256]{2,1,0:T(8,128)(2,1)} copy(bf16[64,8,256]{2,1,0:T(8,128)(2,1)S(1)} %bitcast.6) | data formatting | bytes 524288
  44.1 0.7 %copy.11 = bf16[64,8,256]{2,1,0:T(8,128)(2,1)} copy(bf16[64,8,256]{2,1,0:T(8,128)(2,1)S(1)} %bitcast.5) | data formatting | bytes 524288
Async XLA Ops:
  0.6 2.2 %copy-start = (bf16[8192,256]{1,0:T(8,128)(2,1)S(1)}, bf16[8192,256]{1,0:T(8,128)(2,1)}, u32[]{:S(2)}) copy-start(bf16[8192,256]{1,0:T(8,128)(2,1)} %wk_hbm.1) | copy-start | bytes 12582916
  2.8 1.2 %copy-start.1 = (bf16[256,2048]{1,0:T(8,128)(2,1)S(1)}, bf16[256,2048]{1,0:T(8,128)(2,1)}, u32[]{:S(2)}) copy-start(bf16[256,2048]{1,0:T(8,128)(2,1)} %f_hbm.1) | copy-start | bytes 3145732
  4.0 0.7 %copy-start.2 = (s32[32]{0:T(128)S(1)}, s32[32]{0:T(128)}, u32[]{:S(2)}) copy-start(s32[32]{0:T(128)} %param.9) | copy-start | bytes 388
  4.7 0.7 %copy-start.3 = (s32[32]{0:T(128)S(1)}, s32[32]{0:T(128)}, u32[]{:S(2)}) copy-start(s32[32]{0:T(128)} %param.10) | copy-start | bytes 388
  5.4 0.7 %copy-start.4 = (s32[32]{0:T(128)S(1)}, s32[32]{0:T(128)}, u32[]{:S(2)}) copy-start(s32[32]{0:T(128)} %param.11) | copy-start | bytes 388

commit v2 on v1

--- a/solution.py
+++ b/solution.py
@@ -93,9 +93,9 @@
 
 
 def kernel(
-    dims, f_hbm, wk_hbm, wv_hbm, acc_ref, own_ref, page_ref, k_out, v_out,
-    feats, weights, part, rows_buf, keys, place, k_stage, v_stage,
-    load_sem, w_sem, out_sem, x_send, x_recv, d_send, d_recv, f_send, f_recv,
+    dims, f_hbm, wk_hbm, wv_hbm, acc_hbm, own_hbm, page_hbm, k_out, v_out,
+    feats, weights, part, rows_buf, keys, place, acc_ref, own_ref, page_ref,
+    load_sem, w_sem, id_sem, x_send, x_recv, d_send, d_recv, f_send, f_recv,
     z_send, z_recv, i_send, i_recv,
 ):
     seqs, chunks, draft = dims
@@ -103,7 +103,7 @@
     cols = wk_hbm.shape[1]
     step = rows // chunks
     requests = rows // draft
-    slot_rows = k_stage.shape[0]
+    slot_rows = k_out.shape[0]
     head = lax.axis_index("head")
     seq = lax.axis_index("seq")
     partner = head + 1 - 2 * (head % 2)
@@ -112,6 +112,14 @@
 
     load = pltpu.make_async_copy(f_hbm, feats.at[0], load_sem)
     load.start()
+    id_loads = [
+        pltpu.make_async_copy(src, dst, id_sem.at[n])
+        for n, (src, dst) in enumerate(
+            ((acc_hbm, acc_ref), (own_hbm, own_ref), (page_hbm, page_ref))
+        )
+    ]
+    for id_load in id_loads:
+        id_load.start()
     w_loads = []
     for k in range(4):
         at = pl.ds(pl.multiple_of(blocks[k] * depth, depth), depth)
@@ -170,6 +178,8 @@
     own = remote(feats.at[0], feats.at[1], d_send, d_recv, {"head": partner})
     own.start()
 
+    for id_load in id_loads:
+        id_load.wait()
     spread = (
         lax.broadcasted_iota(jnp.int32, (requests, rows), 1) // draft
         == lax.broadcasted_iota(jnp.int32, (requests, rows), 0)
@@ -246,14 +256,8 @@
     first = placed(0)
     arrive(chunks // 2, chunks)
     cache = (first + placed(1)).astype(jnp.bfloat16)
-    k_stage[...] = cache[:, :cols]
-    v_stage[...] = cache[:, cols:]
-    outs = [
-        pltpu.make_async_copy(k_stage, k_out, out_sem.at[0]),
-        pltpu.make_async_copy(v_stage, v_out, out_sem.at[1]),
-    ]
-    for out in outs:
-        out.start()
+    k_out[...] = cache[:, :cols]
+    v_out[...] = cache[:, cols:]
 
     @pl.loop(0, chunks)
     def _(c):
@@ -265,8 +269,6 @@
     own.wait_send()
     for d in range(1, seqs):
         i_copy(d).wait_send()
-    for out in outs:
-        out.wait()
 
 
 def fused(seqs, draft_features, w_key, w_value, accepted, owner_group, page_slot):
@@ -278,14 +280,14 @@
     chunks = 8
     step = rows // chunks
     dma = pltpu.SemaphoreType.DMA
-    any_spec = pl.BlockSpec(memory_space=pl.ANY)
+    hbm_spec = pl.BlockSpec(memory_space=pltpu.HBM)
     vmem_spec = pl.BlockSpec(memory_space=pltpu.VMEM)
     bf16 = jnp.bfloat16
     key_cache, value_cache = pl.pallas_call(
         functools.partial(kernel, (seqs, chunks, draft)),
         out_shape=(jax.ShapeDtypeStruct((slots * draft, cols), bf16),) * 2,
-        in_specs=[any_spec] * 3 + [vmem_spec] * 3,
-        out_specs=(any_spec, any_spec),
+        in_specs=[hbm_spec] * 6,
+        out_specs=(vmem_spec, vmem_spec),
         scratch_shapes=[
             pltpu.VMEM((4, rows, depth), bf16),
             pltpu.VMEM((4, depth, 2 * cols), bf16),
@@ -293,15 +295,16 @@
             pltpu.VMEM((seqs, rows, 2 * cols), bf16),
             pltpu.VMEM((seqs, 8, rows), jnp.int32),
             pltpu.VMEM((seqs, slots * draft, rows), bf16),
-            pltpu.VMEM((slots * draft, cols), bf16),
-            pltpu.VMEM((slots * draft, cols), bf16),
-            dma, dma((4, 2)), dma((2,)),
+            pltpu.VMEM((1, requests), jnp.int32),
+            pltpu.VMEM((1, requests), jnp.int32),
+            pltpu.VMEM((1, requests), jnp.int32),
+            dma, dma((4, 2)), dma((3,)),
             dma((chunks,)), dma((chunks,)), dma, dma, dma((chunks,)), dma((chunks,)),
             dma((seqs - 1, chunks)), dma((seqs - 1, chunks)),
             dma((seqs - 1,)), dma((seqs - 1,)),
         ],
         compiler_params=pltpu.CompilerParams(
-            collective_id=0, has_side_effects=True, vmem_limit_bytes=48 << 20
+            collective_id=0, has_side_effects=True, vmem_limit_bytes=67043328
         ),
         name="import_rows",
     )(

time: 45 us -> 42 us (0.933)
  local copies, waits for them, and re-layouts: 6.78 us -> 3.34 us
  Pallas kernels: 37.3 us -> 37.9 us
    unnamed x12 -> x2, local copies, waits for them, and re-layouts: 6.78 us -> 3.34 us
    pallas_call x1, Pallas kernels: 37.3 us -> 37.9 us  [fused(): pl.pallas_call(functools.partial(kernel, (seqs, chunks, draft)), out_shap...]
where the time goes in v2:
time: 42 us; the launch traced here: 41.8 us
  Pallas kernels  37.9 us (90%)
  local copies, waits for them, and re-layouts  3.34 us (8%)
  between operations  0.64 us (2%)
    pallas_call x1, Pallas kernels, fused(): pl.pallas_call(functools.partial(kernel, (seqs, chunks, draft)), out_shap...  37.9 us
    unnamed x2, local copies, waits for them, and re-layouts  3.34 us

profile of v2, /device:TPU:0, one launch (start us, length us, event | category | flops | bytes accessed | tf_op | source)
XLA Modules:
  0.0 41.8 jit_solution(5556866637449703611)
XLA Ops:
  0.6 37.9 %import_rows.1 = (bf16[512,256]{1,0:T(8,128)(2,1)}, bf16[512,256]{1,0:T(8,128)(2,1)}) custom-call(bf16[256,2048]{1,0:T(8,128)(2,1)} %f_hbm.1, bf16[8192,256]{1,0:T(8,128)(2,1)} %wk_hbm.1, bf16[8192,256]{1,0:T(8,128)(2,1)} %wv_hbm.1, s32[1,32]{1,0:T(1,128)} %bitcast.7, s32[1,32]{1,0:T(1,128)} %bitcast.8, s32[1,32]{1,0:T(1,128)} %bitcast.9), custom_call_target="tpu_custom_call" | custom-call | tf_op jit(solution)/shard_map/import_rows/pallas_call | solution.py:286
  38.5 1.7 %copy.10 = bf16[64,8,256]{2,1,0:T(8,128)(2,1)} copy(bf16[64,8,256]{2,1,0:T(8,128)(2,1)} %bitcast.6) | data formatting | bytes 524288
  40.2 1.7 %copy.11 = bf16[64,8,256]{2,1,0:T(8,128)(2,1)} copy(bf16[64,8,256]{2,1,0:T(8,128)(2,1)} %bitcast.5) | data formatting | bytes 524288

commit v3 on v2

--- a/solution.py
+++ b/solution.py
@@ -94,7 +94,8 @@
 
 def kernel(
     dims, f_hbm, wk_hbm, wv_hbm, acc_hbm, own_hbm, page_hbm, k_out, v_out,
-    feats, weights, part, rows_buf, keys, place, acc_ref, own_ref, page_ref,
+    raw, feats, weights, part, z_out, z_in, key_out, key_in, place,
+    acc_ref, own_ref, page_ref,
     load_sem, w_sem, id_sem, x_send, x_recv, d_send, d_recv, f_send, f_recv,
     z_send, z_recv, i_send, i_recv,
 ):
@@ -103,23 +104,27 @@
     cols = wk_hbm.shape[1]
     step = rows // chunks
     requests = rows // draft
+    cap = requests // 2
+    share = cap // chunks
+    piece = share * draft
     slot_rows = k_out.shape[0]
+    bf16, f32, i32 = jnp.bfloat16, jnp.float32, jnp.int32
     head = lax.axis_index("head")
     seq = lax.axis_index("seq")
     partner = head + 1 - 2 * (head % 2)
     across = (head + 2) % 4
     blocks = (head, partner, across, (partner + 2) % 4)
 
-    load = pltpu.make_async_copy(f_hbm, feats.at[0], load_sem)
-    load.start()
     id_loads = [
         pltpu.make_async_copy(src, dst, id_sem.at[n])
         for n, (src, dst) in enumerate(
-            ((acc_hbm, acc_ref), (own_hbm, own_ref), (page_hbm, page_ref))
+            ((own_hbm, own_ref), (acc_hbm, acc_ref), (page_hbm, page_ref))
         )
     ]
     for id_load in id_loads:
         id_load.start()
+    load = pltpu.make_async_copy(f_hbm, raw, load_sem)
+    load.start()
     w_loads = []
     for k in range(4):
         at = pl.ds(pl.multiple_of(blocks[k] * depth, depth), depth)
@@ -137,6 +142,29 @@
         pl.semaphore_signal(barrier, inc=1, device_id=peer, device_id_type=MESH)
     for w_load in w_loads:
         w_load.start()
+
+    def iota(shape, dim):
+        return lax.broadcasted_iota(i32, shape, dim)
+
+    def exact(values, table, dims=(((1,), (0,)), ((), ()))):
+        return lax.dot_general(
+            values.astype(bf16), table.astype(bf16), dims, preferred_element_type=f32
+        )
+
+    for id_load in id_loads:
+        id_load.wait()
+    owner = own_ref[...]
+    low = jnp.min(owner, axis=1, keepdims=True)
+    high = jnp.max(owner, axis=1, keepdims=True)
+    mine = (iota((8, requests), 0) == owner).astype(f32)
+    earlier = (iota((requests, requests), 0) < iota((requests, requests), 1)).astype(f32)
+    rank = jnp.sum(mine * exact(mine, earlier), axis=0, keepdims=True).astype(i32)
+    spot = (rank // share) * (2 * share) + rank % share + jnp.where(owner > low, share, 0)
+    spread = (iota((requests, rows), 1) // draft == iota((requests, rows), 0)).astype(f32)
+    wide = exact(jnp.broadcast_to(spot.astype(f32), (8, requests)), spread)
+    goal = wide.astype(i32)[0:1, :] * draft + iota((1, rows), 1) % draft
+    order = (iota((rows, rows), 0) == goal).astype(bf16)
+
     load.wait()
     pl.semaphore_wait(barrier, len(peers))
 
@@ -162,100 +190,95 @@
         )
 
     def z_copy(c, d):
+        at = pl.ds(c * piece, piece)
         return remote(
-            rows_buf.at[0, cut(c), :], rows_buf.at[d, cut(c), :],
+            z_out.at[d - 1, at, :], z_in.at[d, at, :],
             z_send.at[d - 1, c], z_recv.at[d - 1, c], {"seq": (seq + d) % seqs},
         )
 
     def i_copy(d):
         return remote(
-            keys.at[0], keys.at[d], i_send.at[d - 1], i_recv.at[d - 1],
+            key_out.at[d - 1], key_in.at[d], i_send.at[d - 1], i_recv.at[d - 1],
             {"seq": (seq + d) % seqs},
         )
 
-    for c in range(chunks):
-        x_copy(c).start()
+    early = 2
+    for first, last in ((0, early), (early, chunks)):
+        some = slice(first * step, last * step)
+        feats[0, some, :] = jnp.dot(
+            order[some], raw[...], preferred_element_type=f32
+        ).astype(bf16)
+        for c in range(first, last):
+            x_copy(c).start()
     own = remote(feats.at[0], feats.at[1], d_send, d_recv, {"head": partner})
     own.start()
 
-    for id_load in id_loads:
-        id_load.wait()
-    spread = (
-        lax.broadcasted_iota(jnp.int32, (requests, rows), 1) // draft
-        == lax.broadcasted_iota(jnp.int32, (requests, rows), 0)
-    ).astype(jnp.bfloat16)
-
-    def widen(ref):
-        values = jnp.broadcast_to(ref[...].astype(jnp.float32), (8, requests))
-        wide = jnp.dot(
-            values.astype(jnp.bfloat16), spread, preferred_element_type=jnp.float32
-        )
-        return wide.astype(jnp.int32)
-
-    within = lax.broadcasted_iota(jnp.int32, (8, rows), 1) % draft
-    keys[0] = jnp.where(
-        within < widen(acc_ref),
-        widen(own_ref) * slot_rows + widen(page_ref) * draft + within,
-        -1,
-    )
-    for d in range(1, seqs):
-        i_copy(d).start()
+    page = jnp.broadcast_to(page_ref[...].astype(f32), (8, requests))
+    live = jnp.broadcast_to(acc_ref[...].astype(f32), (8, requests))
+    within = iota((8, cap * draft), 1) % draft
+    last_dims = (((1,), (1,)), ((), ()))
+    for d in range(seqs):
+        taken = (
+            (owner == (seq + d) % seqs) & (rank == iota((cap * draft, requests), 0) // draft)
+        ).astype(f32)
+        key = jnp.where(
+            within < exact(live, taken, last_dims).astype(i32),
+            exact(page, taken, last_dims).astype(i32) * draft + within,
+            -1,
+        )
+        if d == 0:
+            key_in[0] = key
+        else:
+            key_out[d - 1] = key
+            i_copy(d).start()
 
     w_loads[0].wait()
     w_loads[1].wait()
-    part[...] = jnp.dot(feats[0], weights[0], preferred_element_type=jnp.float32)
+    part[...] = jnp.dot(feats[0], weights[0], preferred_element_type=f32)
     own.wait_recv()
     w_loads[2].wait()
     w_loads[3].wait()
-    part[...] += jnp.dot(feats[1], weights[1], preferred_element_type=jnp.float32)
+    part[...] += jnp.dot(feats[1], weights[1], preferred_element_type=f32)
 
     for d in range(seqs):
         if d > 0:
             i_copy(d).wait_recv()
-        target = keys[d][0:1, :] - seq * slot_rows
-        place[d] = (
-            lax.broadcasted_iota(jnp.int32, (slot_rows, rows), 0) == target
-        ).astype(jnp.bfloat16)
+        place[:, d * cap * draft : (d + 1) * cap * draft] = (
+            iota((slot_rows, cap * draft), 0) == key_in[d][0:1, :]
+        ).astype(bf16)
     for w_load in w_loads[4:]:
         w_load.wait()
 
     @pl.loop(0, chunks)
     def _(c):
-        at = cut(pl.multiple_of(c, 1))
+        at = cut(c)
         x_copy(c).wait_recv()
         forward(c).start()
         total = part[at, :] + jnp.dot(
-            feats[2, at, :], weights[2], preferred_element_type=jnp.float32
+            feats[2, at, :], weights[2], preferred_element_type=f32
         )
         forward(c).wait_recv()
-        total += jnp.dot(feats[3, at, :], weights[3], preferred_element_type=jnp.float32)
-        rows_buf[0, at, :] = total.astype(jnp.bfloat16)
+        total += jnp.dot(feats[3, at, :], weights[3], preferred_element_type=f32)
+        of_low, of_high = total[:piece], total[piece:]
+        to = pl.ds(c * piece, piece)
+        for d in [*range(1, seqs), 0]:
+            target = (seq + d) % seqs
+            chosen = jnp.where(
+                low == target, of_low, jnp.where(high == target, of_high, 0.0)
+            ).astype(bf16)
+            if d == 0:
+                z_in[0, to, :] = chosen
+            else:
+                z_out[d - 1, to, :] = chosen
+                z_copy(c, d).start()
+
+    @pl.loop(0, chunks)
+    def _(c):
         for d in range(1, seqs):
-            z_copy(c, d).start()
-
-    half = rows // 2
-
-    def placed(h):
-        total = None
-        for d in range(seqs):
-            more = jnp.dot(
-                place[d, :, h * half : (h + 1) * half],
-                rows_buf[d, h * half : (h + 1) * half, :],
-                preferred_element_type=jnp.float32,
-            )
-            total = more if total is None else total + more
-        return total
-
-    def arrive(first, last):
-        @pl.loop(first, last)
-        def _(c):
-            for d in range(1, seqs):
-                z_copy(c, d).wait_recv()
-
-    arrive(0, chunks // 2)
-    first = placed(0)
-    arrive(chunks // 2, chunks)
-    cache = (first + placed(1)).astype(jnp.bfloat16)
+            z_copy(c, d).wait_recv()
+
+    arrived = z_in[...].reshape(seqs * cap * draft, 2 * cols)
+    cache = jnp.dot(place[...], arrived, preferred_element_type=f32).astype(bf16)
     k_out[...] = cache[:, :cols]
     v_out[...] = cache[:, cols:]
 
@@ -278,7 +301,9 @@
     draft = rows // requests
     slots = max(2, 2 * requests // seqs) * seqs
     chunks = 8
-    step = rows // chunks
+    sent = rows // 2
+    if 2 * (slots // seqs) != requests:
+        return plain(draft_features, w_key, w_value, accepted, owner_group, page_slot)
     dma = pltpu.SemaphoreType.DMA
     hbm_spec = pl.BlockSpec(memory_space=pltpu.HBM)
     vmem_spec = pl.BlockSpec(memory_space=pltpu.VMEM)
@@ -289,12 +314,15 @@
         in_specs=[hbm_spec] * 6,
         out_specs=(vmem_spec, vmem_spec),
         scratch_shapes=[
+            pltpu.VMEM((rows, depth), bf16),
             pltpu.VMEM((4, rows, depth), bf16),
             pltpu.VMEM((4, depth, 2 * cols), bf16),
             pltpu.VMEM((rows, 2 * cols), jnp.float32),
-            pltpu.VMEM((seqs, rows, 2 * cols), bf16),
-            pltpu.VMEM((seqs, 8, rows), jnp.int32),
-            pltpu.VMEM((seqs, slots * draft, rows), bf16),
+            pltpu.VMEM((seqs - 1, sent, 2 * cols), bf16),
+            pltpu.VMEM((seqs, sent, 2 * cols), bf16),
+            pltpu.VMEM((seqs - 1, 8, sent), jnp.int32),
+            pltpu.VMEM((seqs, 8, sent), jnp.int32),
+            pltpu.VMEM((slots * draft, seqs * sent), bf16),
             pltpu.VMEM((1, requests), jnp.int32),
             pltpu.VMEM((1, requests), jnp.int32),
             pltpu.VMEM((1, requests), jnp.int32),
@@ -304,13 +332,18 @@
             dma((seqs - 1,)), dma((seqs - 1,)),
         ],
         compiler_params=pltpu.CompilerParams(
-            collective_id=0, has_side_effects=True, vmem_limit_bytes=67043328
+            collective_id=0, has_side_effects=True, vmem_limit_bytes=48 << 20
         ),
         name="import_rows",
     )(
-        draft_features, w_key, w_value,
-        accepted.reshape(1, requests), owner_group.reshape(1, requests),
-        page_slot.reshape(1, requests),
+        *(
+            pltpu.with_memory_space_constraint(x, pltpu.HBM)
+            for x in (
+                draft_features, w_key, w_value,
+                accepted.reshape(1, requests), owner_group.reshape(1, requests),
+                page_slot.reshape(1, requests),
+            )
+        )
     )
     return (
         key_cache.reshape(slots, draft, cols),

time: 42 us -> 38 us (0.905)
  Pallas kernels: 37.9 us -> 35.8 us
  local copies, waits for them, and re-layouts: 3.34 us -> 1.41 us
    pallas_call x1, Pallas kernels: 37.9 us -> 35.8 us  [fused(): pl.pallas_call(functools.partial(kernel, (seqs, chunks, draft)), out_shap...]
    unnamed x2, local copies, waits for them, and re-layouts: 3.34 us -> 1.41 us
where the time goes in v3:
time: 38 us; the launch traced here: 37.9 us
  Pallas kernels  35.8 us (94%)
  local copies, waits for them, and re-layouts  1.41 us (4%)
  between operations  0.64 us (2%)
    pallas_call x1, Pallas kernels, fused(): pl.pallas_call(functools.partial(kernel, (seqs, chunks, draft)), out_shap...  35.8 us
    unnamed x2, local copies, waits for them, and re-layouts  1.41 us

profile of v3, /device:TPU:0, one launch (start us, length us, event | category | flops | bytes accessed | tf_op | source)
XLA Modules:
  0.0 37.9 jit_solution(17967286559982685243)
XLA Ops:
  0.6 35.8 %import_rows.1 = (bf16[512,256]{1,0:T(8,128)(2,1)S(1)}, bf16[512,256]{1,0:T(8,128)(2,1)S(1)}) custom-call(bf16[256,2048]{1,0:T(8,128)(2,1)} %f_hbm.1, bf16[8192,256]{1,0:T(8,128)(2,1)} %wk_hbm.1, bf16[8192,256]{1,0:T(8,128)(2,1)} %wv_hbm.1, s32[1,32]{1,0:T(1,128)} %bitcast.7, s32[1,32]{1,0:T(1,128)} %bitcast.8, s32[1,32]{1,0:T(1,128)} %bitcast.9), custom_call_target="tpu_custom_call" | custom-call | tf_op jit(solution)/shard_map/import_rows/pallas_call | solution.py:311
  36.5 0.7 %copy.10 = bf16[64,8,256]{2,1,0:T(8,128)(2,1)} copy(bf16[64,8,256]{2,1,0:T(8,128)(2,1)S(1)} %bitcast.6) | data formatting | bytes 524288
  37.2 0.7 %copy.11 = bf16[64,8,256]{2,1,0:T(8,128)(2,1)} copy(bf16[64,8,256]{2,1,0:T(8,128)(2,1)S(1)} %bitcast.5) | data formatting | bytes 524288

commit v4 on v3

--- a/solution.py
+++ b/solution.py
@@ -94,7 +94,7 @@
 
 def kernel(
     dims, f_hbm, wk_hbm, wv_hbm, acc_hbm, own_hbm, page_hbm, k_out, v_out,
-    raw, feats, weights, part, z_out, z_in, key_out, key_in, place,
+    raw, feats, weights, part, z_out, z_in, key_out, key_in, place, cache,
     acc_ref, own_ref, page_ref,
     load_sem, w_sem, id_sem, x_send, x_recv, d_send, d_recv, f_send, f_recv,
     z_send, z_recv, i_send, i_recv,
@@ -107,6 +107,8 @@
     cap = requests // 2
     share = cap // chunks
     piece = share * draft
+    group = cap * draft // 2
+    turns = chunks // 2
     slot_rows = k_out.shape[0]
     bf16, f32, i32 = jnp.bfloat16, jnp.float32, jnp.int32
     head = lax.axis_index("head")
@@ -166,7 +168,6 @@
     order = (iota((rows, rows), 0) == goal).astype(bf16)
 
     load.wait()
-    pl.semaphore_wait(barrier, len(peers))
 
     def remote(src, dst, send_sem, recv_sem, peer):
         return pltpu.make_async_remote_copy(
@@ -191,8 +192,9 @@
 
     def z_copy(c, d):
         at = pl.ds(c * piece, piece)
+        there = pl.ds((c % turns) * piece, piece)
         return remote(
-            z_out.at[d - 1, at, :], z_in.at[d, at, :],
+            z_out.at[d - 1, at, :], z_in.at[c // turns, d, there, :],
             z_send.at[d - 1, c], z_recv.at[d - 1, c], {"seq": (seq + d) % seqs},
         )
 
@@ -208,6 +210,8 @@
         feats[0, some, :] = jnp.dot(
             order[some], raw[...], preferred_element_type=f32
         ).astype(bf16)
+        if first == 0:
+            pl.semaphore_wait(barrier, len(peers))
         for c in range(first, last):
             x_copy(c).start()
     own = remote(feats.at[0], feats.at[1], d_send, d_recv, {"head": partner})
@@ -243,44 +247,61 @@
     for d in range(seqs):
         if d > 0:
             i_copy(d).wait_recv()
-        place[:, d * cap * draft : (d + 1) * cap * draft] = (
-            iota((slot_rows, cap * draft), 0) == key_in[d][0:1, :]
-        ).astype(bf16)
+        placing = (iota((slot_rows, cap * draft), 0) == key_in[d][0:1, :]).astype(bf16)
+        for g in range(2):
+            place[g, :, d * group : (d + 1) * group] = placing[:, g * group : (g + 1) * group]
     for w_load in w_loads[4:]:
         w_load.wait()
 
-    @pl.loop(0, chunks)
-    def _(c):
-        at = cut(c)
+    def meet(c):
         x_copy(c).wait_recv()
         forward(c).start()
+
+    def cross(c):
+        at = cut(c)
+        part[at, :] += jnp.dot(feats[2, at, :], weights[2], preferred_element_type=f32)
+
+    def finish(c):
+        at = cut(c)
+        forward(c).wait_recv()
         total = part[at, :] + jnp.dot(
-            feats[2, at, :], weights[2], preferred_element_type=f32
-        )
-        forward(c).wait_recv()
-        total += jnp.dot(feats[3, at, :], weights[3], preferred_element_type=f32)
+            feats[3, at, :], weights[3], preferred_element_type=f32
+        )
         of_low, of_high = total[:piece], total[piece:]
-        to = pl.ds(c * piece, piece)
         for d in [*range(1, seqs), 0]:
             target = (seq + d) % seqs
             chosen = jnp.where(
                 low == target, of_low, jnp.where(high == target, of_high, 0.0)
             ).astype(bf16)
             if d == 0:
-                z_in[0, to, :] = chosen
+                z_in[c // turns, 0, pl.ds((c % turns) * piece, piece), :] = chosen
             else:
-                z_out[d - 1, to, :] = chosen
+                z_out[d - 1, pl.ds(c * piece, piece), :] = chosen
                 z_copy(c, d).start()
 
-    @pl.loop(0, chunks)
+    meet(0)
+    cross(0)
+
+    @pl.loop(1, chunks)
     def _(c):
-        for d in range(1, seqs):
-            z_copy(c, d).wait_recv()
-
-    arrived = z_in[...].reshape(seqs * cap * draft, 2 * cols)
-    cache = jnp.dot(place[...], arrived, preferred_element_type=f32).astype(bf16)
-    k_out[...] = cache[:, :cols]
-    v_out[...] = cache[:, cols:]
+        meet(c)
+        finish(c - 1)
+        cross(c)
+
+    finish(chunks - 1)
+
+    def arrive(first, last):
+        @pl.loop(first, last)
+        def _(c):
+            for d in range(1, seqs):
+                z_copy(c, d).wait_recv()
+
+    def placed(g):
+        arrived = z_in[g].reshape(seqs * group, 2 * cols)
+        return jnp.dot(place[g], arrived, preferred_element_type=f32)
+
+    arrive(0, turns)
+    cache[...] = placed(0)
 
     @pl.loop(0, chunks)
     def _(c):
@@ -292,6 +313,21 @@
     own.wait_send()
     for d in range(1, seqs):
         i_copy(d).wait_send()
+    arrive(turns, chunks)
+    both = (cache[...] + placed(1)).astype(bf16)
+    k_out[...] = both[:, :cols]
+    v_out[...] = both[:, cols:]
+
+
+def store(k_in, v_in, k_out, v_out, sems):
+    copies = [
+        pltpu.make_async_copy(k_in, k_out, sems.at[0]),
+        pltpu.make_async_copy(v_in, v_out, sems.at[1]),
+    ]
+    for copy in copies:
+        copy.start()
+    for copy in copies:
+        copy.wait()
 
 
 def fused(seqs, draft_features, w_key, w_value, accepted, owner_group, page_slot):
@@ -319,10 +355,11 @@
             pltpu.VMEM((4, depth, 2 * cols), bf16),
             pltpu.VMEM((rows, 2 * cols), jnp.float32),
             pltpu.VMEM((seqs - 1, sent, 2 * cols), bf16),
-            pltpu.VMEM((seqs, sent, 2 * cols), bf16),
+            pltpu.VMEM((2, seqs, sent // 2, 2 * cols), bf16),
             pltpu.VMEM((seqs - 1, 8, sent), jnp.int32),
             pltpu.VMEM((seqs, 8, sent), jnp.int32),
-            pltpu.VMEM((slots * draft, seqs * sent), bf16),
+            pltpu.VMEM((2, slots * draft, seqs * sent // 2), bf16),
+            pltpu.VMEM((slots * draft, 2 * cols), jnp.float32),
             pltpu.VMEM((1, requests), jnp.int32),
             pltpu.VMEM((1, requests), jnp.int32),
             pltpu.VMEM((1, requests), jnp.int32),
@@ -345,6 +382,15 @@
             )
         )
     )
+    key_cache, value_cache = pl.pallas_call(
+        store,
+        out_shape=(jax.ShapeDtypeStruct((slots * draft, cols), bf16),) * 2,
+        in_specs=[vmem_spec] * 2,
+        out_specs=(hbm_spec, hbm_spec),
+        scratch_shapes=[dma((2,))],
+        compiler_params=pltpu.CompilerParams(vmem_limit_bytes=8 << 20),
+        name="store",
+    )(key_cache, value_cache)
     return (
         key_cache.reshape(slots, draft, cols),
         value_cache.reshape(slots, draft, cols),

time: 38 us -> 37.4 us (0.984)
  local copies, waits for them, and re-layouts: 1.41 us -> 0 us
  Pallas kernels: 35.8 us -> 36.6 us
    unnamed x2 -> x0, local copies, waits for them, and re-layouts: 1.41 us -> none
    pallas_call x0 -> x1, Pallas kernels: none -> 0.81 us  [fused(): pl.pallas_call(store, out_shape=(jax.ShapeDtypeStruct((slots * draft, col...]
where the time goes in v4:
time: 37.4 us; the launch traced here: 37.3 us
  Pallas kernels  36.6 us (98%)
  between operations  0.64 us (2%)
    pallas_call x1, Pallas kernels, fused(): pl.pallas_call(functools.partial(kernel, (seqs, chunks, draft)), out_shap...  35.8 us
    pallas_call x1, Pallas kernels, fused(): pl.pallas_call(store, out_shape=(jax.ShapeDtypeStruct((slots * draft, col...  0.81 us

profile of v4, /device:TPU:0, one launch (start us, length us, event | category | flops | bytes accessed | tf_op | source)
XLA Modules:
  0.0 37.3 jit_solution(14629226211445133394)
XLA Ops:
  0.6 35.8 %import_rows.1 = (bf16[512,256]{1,0:T(8,128)(2,1)S(1)}, bf16[512,256]{1,0:T(8,128)(2,1)S(1)}) custom-call(bf16[256,2048]{1,0:T(8,128)(2,1)} %f_hbm.1, bf16[8192,256]{1,0:T(8,128)(2,1)} %wk_hbm.1, bf16[8192,256]{1,0:T(8,128)(2,1)} %wv_hbm.1, s32[1,32]{1,0:T(1,128)} %bitcast.5, s32[1,32]{1,0:T(1,128)} %bitcast.6, s32[1,32]{1,0:T(1,128)} %bitcast.7), custom_call_target="tpu_custom_call" | custom-call | tf_op jit(solution)/shard_map/import_rows/pallas_call | solution.py:347
  36.5 0.8 %store.1 = (bf16[512,256]{1,0:T(8,128)(2,1)}, bf16[512,256]{1,0:T(8,128)(2,1)}) custom-call(bf16[512,256]{1,0:T(8,128)(2,1)S(1)} %get-tuple-element.6.k_in, bf16[512,256]{1,0:T(8,128)(2,1)S(1)} %get-tuple-element.7.v_in), custom_call_target="tpu_custom_call" | custom-call | tf_op jit(solution)/shard_map/store/pallas_call | solution.py:385

commit v5 on v4

--- a/solution.py
+++ b/solution.py
@@ -268,12 +268,14 @@
             feats[3, at, :], weights[3], preferred_element_type=f32
         )
         of_low, of_high = total[:piece], total[piece:]
-        for d in [*range(1, seqs), 0]:
+        upper = (2 * seq) // seqs
+        far = [upper * k + (1 - upper) * (seqs - k) for k in range(1, seqs)]
+        for d in [*far, 0]:
             target = (seq + d) % seqs
             chosen = jnp.where(
                 low == target, of_low, jnp.where(high == target, of_high, 0.0)
             ).astype(bf16)
-            if d == 0:
+            if isinstance(d, int):
                 z_in[c // turns, 0, pl.ds((c % turns) * piece, piece), :] = chosen
             else:
                 z_out[d - 1, pl.ds(c * piece, piece), :] = chosen

time: 37.4 us -> 37.4 us (level)
  no operation moved by 1% of the time
where the time goes in v5:
time: 37.4 us; the launch traced here: 37.3 us
  Pallas kernels  36.6 us (98%)
  between operations  0.64 us (2%)
    pallas_call x1, Pallas kernels, fused(): pl.pallas_call(functools.partial(kernel, (seqs, chunks, draft)), out_shap...  35.8 us
    pallas_call x1, Pallas kernels, fused(): pl.pallas_call(store, out_shape=(jax.ShapeDtypeStruct((slots * draft, col...  0.81 us

profile of v5, /device:TPU:0, one launch (start us, length us, event | category | flops | bytes accessed | tf_op | source)
XLA Modules:
  0.0 37.3 jit_solution(188124681399517426)
XLA Ops:
  0.6 35.8 %import_rows.1 = (bf16[512,256]{1,0:T(8,128)(2,1)S(1)}, bf16[512,256]{1,0:T(8,128)(2,1)S(1)}) custom-call(bf16[256,2048]{1,0:T(8,128)(2,1)} %f_hbm.1, bf16[8192,256]{1,0:T(8,128)(2,1)} %wk_hbm.1, bf16[8192,256]{1,0:T(8,128)(2,1)} %wv_hbm.1, s32[1,32]{1,0:T(1,128)} %bitcast.5, s32[1,32]{1,0:T(1,128)} %bitcast.6, s32[1,32]{1,0:T(1,128)} %bitcast.7), custom_call_target="tpu_custom_call" | custom-call | tf_op jit(solution)/shard_map/import_rows/pallas_call | solution.py:349
  36.5 0.8 %store.1 = (bf16[512,256]{1,0:T(8,128)(2,1)}, bf16[512,256]{1,0:T(8,128)(2,1)}) custom-call(bf16[512,256]{1,0:T(8,128)(2,1)S(1)} %get-tuple-element.6.k_in, bf16[512,256]{1,0:T(8,128)(2,1)S(1)} %get-tuple-element.7.v_in), custom_call_target="tpu_custom_call" | custom-call | tf_op jit(solution)/shard_map/store/pallas_call | solution.py:387
